TPU v7x, 32 devices: a whole 2x2x4 slice. The times are simulated.
32 devices in a mesh: blocks: 2 (over y), gz: 8 (over z, x), gy: 2 (over core).
Axes of the slice: x: 2, y: 2, z: 4, core: 2. Of those that a mesh axis runs over, the one named last changes fastest.
Arguments:
- view_a: float32 [256, 32, 512], P(('blocks', 'gz'), 'gy'), parts along dimension 0, may hold values from 0.5 to 2
- view_b_own: float32 [1024, 32, 128], P(('blocks', 'gz'), 'gy'), parts along dimension 0, may hold values from 0.5 to 2
- spread_a: float32 [3, 31], replicated, may hold values from 0.05 to 1
- spread_b: float32 [3, 31], replicated, may hold values from 0.05 to 1
Outputs:
- estimate: float32 [256, 32, 512], P(('blocks', 'gz'), 'gy'), parts along dimension 0
There are 2 independent parts, one for each index of `blocks`. A program takes and returns all parts, laid end to end along the dimension named above; an argument that names none is the same for every part. Nothing has to cross between parts.
All inputs are finite; a program needn't handle non-finite values.
Results may differ from a plain program's by a relative error of at most 0.0001.
Values sent between devices are 32-bit elements; how exact they have to be, the bound alone decides.
A program may use at most 64 MiB of HBM per device.

v0:
```python
import functools

import jax
import jax.numpy as jnp
from jax import lax
from jax.experimental import pallas as pl
from jax.experimental.pallas import tpu as pltpu
from jax.sharding import PartitionSpec as P

LANES = 128
QUARTERS = 4


def padded(cells, sides, width):
    for axis, dim in sides:
        count = lax.axis_size(axis)
        ends = count - 1
        head = lax.slice_in_dim(cells, 0, width, axis=dim)
        tail = lax.slice_in_dim(cells, cells.shape[dim] - width, cells.shape[dim], axis=dim)
        cells = jnp.concatenate(
            [
                lax.ppermute(tail, axis, [(i, (i + 1) % count) for i in range(ends)]),
                cells,
                lax.ppermute(head, axis, [((i + 1) % count, i) for i in range(ends)]),
            ],
            axis=dim,
        )
    return cells


def band_table(weights, count_in, count_out, offset):
    source = jnp.arange(count_in, dtype=jnp.int32)[:, None]
    target = jnp.arange(count_out, dtype=jnp.int32)[None, :]
    spread = source - target + offset
    table = jnp.zeros((count_in, count_out), jnp.float32)
    for place in range(weights.shape[0]):
        table = table + jnp.where(spread == place, weights[place], jnp.float32(0.0))
    return table


def blur(volume, kernels):
    count_z, count_y, count_x = volume.shape
    radius = (kernels.shape[1] - 1) // 2
    table_x = band_table(kernels[2], count_x, count_x, radius)
    along_x = jnp.einsum("zyx,xw->zyw", volume, table_x, precision=lax.Precision.HIGHEST)
    table_y = band_table(kernels[1], count_y + 2 * radius, count_y, 0)
    widened = padded(along_x, (("gy", 1),), radius)
    narrow_y = jnp.einsum("zyx,yw->zwx", widened, table_y, precision=lax.Precision.HIGHEST)
    along_y = padded(narrow_y, (("gz", 0),), radius)
    table_z = band_table(kernels[0], count_z + 2 * radius, count_z, 0)
    return jnp.einsum("zyx,zw->wyx", along_y, table_z, precision=lax.Precision.HIGHEST)


def shards(view_a, view_b_own, spread_a, spread_b):
    arrived = lax.all_to_all(view_b_own, "gz", split_axis=2, concat_axis=0, tiled=True)
    view_b = jnp.transpose(arrived, (2, 1, 0))[:, :, ::-1]
    blur_a = spread_a / jnp.sum(spread_a, axis=1, keepdims=True)
    blur_b = spread_b / jnp.sum(spread_b, axis=1, keepdims=True)
    estimate = 0.5 * (view_a + view_b)
    for measured, kernels in ((view_a, blur_a), (view_b, blur_b)):
        quotient = measured / blur(estimate, kernels)
        estimate = estimate * blur(quotient, kernels[:, ::-1])
    return estimate


def block_transpose(parts, width):
    lane = lax.broadcasted_iota(jnp.int32, parts[0].shape, 1)
    for step in (2, 1):
        shift = step * width
        low = lax.rem(lane // shift, 2) == 0
        out = list(parts)
        for first in range(QUARTERS):
            if first & step:
                continue
            second = first + step
            out[first] = jnp.where(low, parts[first], pltpu.roll(parts[second], shift, 1))
            out[second] = jnp.where(low, pltpu.roll(parts[first], LANES - shift, 1), parts[second])
        parts = out
    return parts


def split(values):
    high = values.astype(jnp.bfloat16)
    return high, (values - high.astype(jnp.float32)).astype(jnp.bfloat16)


def dot(a, b):
    return jnp.dot(a, b, preferred_element_type=jnp.float32)


def deconvolve(
    va_ref, vb_ref, sa_ref, sb_ref, out_ref,
    send_a, recv_a, recv_b, view_a, view_b, estimate, blurred, work, halo_left, halo_right,
    send_e, recv_e, tz_high, tz_low, ty_high, ty_low,
    a_send_sem, a_recv_sem, b_sem, h_send_sem, h_recv_sem, e_send_sem, e_recv_sem,
):
    f32 = jnp.float32
    groups = lax.axis_size("gz")
    devices = 2 * groups
    block = lax.axis_index("blocks")
    gz, gy = lax.axis_index("gz"), lax.axis_index("gy")
    me = 2 * gz + gy
    slab = 2 * (groups - 1 - gz) + gy
    deep, tall, _ = va_ref.shape
    wide, full_y, full_z = view_a.shape
    taps = sa_ref.shape[1]
    radius = (taps - 1) // 2
    rows_y = tall // QUARTERS
    spreads = (sa_ref, sb_ref)

    def slab_of(device):
        return 2 * (groups - 1 - device // 2) + lax.rem(device, 2)

    def at(device):
        return (block, device // 2, lax.rem(device, 2))

    barrier = pltpu.get_barrier_semaphore()
    for hop in range(1, devices):
        pl.semaphore_signal(
            barrier, inc=1, device_id=at(lax.rem(me + hop, devices)), device_id_type=pl.DeviceIdType.MESH
        )

    for y in range(rows_y):
        for column in range(va_ref.shape[2] // LANES):
            parts = [
                va_ref[:, q * rows_y + y, column * LANES:(column + 1) * LANES] for q in range(QUARTERS)
            ]
            for k, part in enumerate(block_transpose(parts, wide)):
                send_a[QUARTERS * column + k, y] = part

    pl.semaphore_wait(barrier, devices - 1)

    half = pltpu.make_async_remote_copy(
        src_ref=vb_ref.at[pl.ds(wide * gy, wide)],
        dst_ref=recv_b,
        send_sem=b_sem.at[0],
        recv_sem=b_sem.at[1],
        device_id=(block, gz, 1 - gy),
        device_id_type=pl.DeviceIdType.MESH,
    )
    half.start()
    copies_a = []
    for hop in range(1, devices):
        target = lax.rem(me + hop, devices)
        copy = pltpu.make_async_remote_copy(
            src_ref=send_a.at[slab_of(target)],
            dst_ref=recv_a.at[gy, :, pl.ds(pl.multiple_of(gz * deep, 8), deep)],
            send_sem=a_send_sem.at[hop],
            recv_sem=a_recv_sem.at[hop],
            device_id=at(target),
            device_id_type=pl.DeviceIdType.MESH,
        )
        copy.start()
        copies_a.append(copy)
    recv_a[gy, :, pl.ds(pl.multiple_of(gz * deep, 8), deep)] = send_a[slab]

    row = lax.broadcasted_iota(jnp.int32, (full_z, LANES), 0)
    col = lax.broadcasted_iota(jnp.int32, (full_z, LANES), 1)
    for which, spread in enumerate(spreads):
        total = f32(1.0)
        for axis in range(3):
            line = spread[axis, 0]
            for tap in range(1, taps):
                line = line + spread[axis, tap]
            total = total * line
        for flipped in range(2):
            index = 2 * which + flipped
            sign = -1 if flipped else 1
            offset = sign * (row - col) + radius
            table = jnp.zeros((full_z, LANES), f32)
            for tap in range(taps):
                table = jnp.where(offset == tap, spread[0, tap], table)
            table = table / jnp.full((full_z, LANES), total, f32)
            tz_high[index], tz_low[index] = split(table)
            offset = jnp.where(row // full_y == col // full_y, sign * (col - row) + radius, -1)
            table = jnp.zeros((LANES, LANES), f32)
            for tap in range(taps):
                table = jnp.where(offset == tap, spread[1, tap], table)
            ty_high[index], ty_low[index] = split(table)

    mine, other = pl.multiple_of(gy * tall, 8), pl.multiple_of((1 - gy) * tall, 8)
    for x in range(wide):
        view_b[x, pl.ds(mine, tall)] = vb_ref[2 * wide - 1 - wide * gy - x]
    half.wait()
    for x in range(wide):
        view_b[x, pl.ds(other, tall)] = recv_b[wide - 1 - x]

    for copy in copies_a:
        copy.wait_recv()
    for side in range(2):
        for y in range(rows_y):
            turned = recv_a[side, y].T
            for q in range(QUARTERS):
                view_a[:, side * tall + q * rows_y + y, :] = turned[q * wide:(q + 1) * wide]

    planes = LANES // full_y
    chunks = wide // planes

    def along_zy(values, index):
        high, low = split(values.reshape(LANES, full_z))
        zh = tz_high[index]
        done = dot(high, zh) + (dot(low, zh) + dot(high, tz_low[index]))
        high, low = split(done)
        yh = ty_high[index]
        done = dot(yh, high) + (dot(yh, low) + dot(ty_low[index], high))
        return done.reshape(planes, full_y, full_z)

    has_left, has_right = slab > 0, slab < devices - 1

    def device_of(place):
        return (block, groups - 1 - place // 2, lax.rem(place, 2))

    left, right = device_of(jnp.maximum(slab - 1, 0)), device_of(jnp.minimum(slab + 1, devices - 1))

    def x_taps(turn, spread, flipped, source, first, outputs, fresh):
        count = source.shape[0]

        def body(part, carry):
            ys = pl.ds(pl.multiple_of(part * 8, 8), 8)
            weights = [spread[2, taps - 1 - tap if flipped else tap] for tap in range(taps)]
            for x in outputs:
                total = None if fresh else blurred[x, ys]
                for tap in range(taps):
                    place = x + tap - radius - first
                    if 0 <= place < count:
                        term = weights[tap] * source[place, ys]
                        total = term if total is None else total + term
                blurred[x, ys] = total
            return carry

        lax.fori_loop(0, full_y // 8, body, 0)

    def blur(turn, which, flipped, values):
        index = 2 * which + flipped
        spread = spreads[which]
        held = work.at[turn]
        to_left = pltpu.make_async_remote_copy(
            src_ref=held.at[pl.ds(0, radius)],
            dst_ref=halo_right.at[turn],
            send_sem=h_send_sem.at[turn, 0],
            recv_sem=h_recv_sem.at[turn, 0],
            device_id=left,
            device_id_type=pl.DeviceIdType.MESH,
        )
        to_right = pltpu.make_async_remote_copy(
            src_ref=held.at[pl.ds(wide - radius, radius)],
            dst_ref=halo_left.at[turn],
            send_sem=h_send_sem.at[turn, 1],
            recv_sem=h_recv_sem.at[turn, 1],
            device_id=right,
            device_id_type=pl.DeviceIdType.MESH,
        )
        for chunk in range(chunks):
            span = pl.ds(chunk * planes, planes)
            held[span] = along_zy(values(span), index)
            if chunk == (radius - 1) // planes:
                pl.when(has_left)(to_left.start)
        pl.when(has_right)(to_right.start)
        x_taps(turn, spread, flipped, held, 0, range(wide), True)

        @pl.when(has_left)
        def _():
            to_right.wait_recv()
            x_taps(turn, spread, flipped, halo_left.at[turn], -radius, range(radius), False)

        @pl.when(has_right)
        def _():
            to_left.wait_recv()
            x_taps(turn, spread, flipped, halo_right.at[turn], wide, range(wide - radius, wide), False)

        pl.when(has_left)(to_left.wait_send)
        pl.when(has_right)(to_right.wait_send)

    def start_values(span):
        estimate[span] = 0.5 * (view_a[span] + view_b[span])
        return estimate[span]

    def next_values(span):
        estimate[span] = estimate[span] * blurred[span]
        return estimate[span]

    blur(0, 0, 0, start_values)
    blur(1, 0, 1, lambda span: view_a[span] / blurred[span])
    blur(2, 1, 0, next_values)
    blur(3, 1, 1, lambda span: view_b[span] / blurred[span])
    for chunk in range(chunks):
        next_values(pl.ds(chunk * planes, planes))

    for side in range(2):
        for y in range(rows_y):
            lines = [estimate[:, side * tall + q * rows_y + y, :] for q in range(QUARTERS)]
            send_e[side, y] = jnp.concatenate(lines, axis=0).T
    copies_e = []
    for hop in range(1, devices):
        target = lax.rem(me + hop, devices)
        copy = pltpu.make_async_remote_copy(
            src_ref=send_e.at[lax.rem(target, 2), :, pl.ds(pl.multiple_of(target // 2 * deep, 8), deep)],
            dst_ref=recv_e.at[slab],
            send_sem=e_send_sem.at[hop],
            recv_sem=e_recv_sem.at[hop],
            device_id=at(target),
            device_id_type=pl.DeviceIdType.MESH,
        )
        copy.start()
        copies_e.append(copy)
    recv_e[slab] = send_e[gy, :, pl.ds(pl.multiple_of(gz * deep, 8), deep)]
    for copy in copies_e:
        copy.wait_recv()
    for y in range(rows_y):
        for column in range(va_ref.shape[2] // LANES):
            parts = [recv_e[QUARTERS * column + k, y] for k in range(QUARTERS)]
            for q, part in enumerate(block_transpose(parts, wide)):
                out_ref[q * rows_y + y, :, column * LANES:(column + 1) * LANES] = part
    for copy in copies_a + copies_e:
        copy.wait_send()


def slab_shards(view_a, view_b_own, spread_a, spread_b):
    groups = lax.axis_size("gz")
    deep, tall, long_x = view_a.shape
    devices = 2 * groups
    wide = long_x // devices
    full_y, full_z = 2 * tall, view_b_own.shape[2]
    taps = spread_a.shape[1]
    radius = (taps - 1) // 2
    f32, bf16 = jnp.float32, jnp.bfloat16
    volume = pltpu.VMEM((wide, full_y, full_z), f32)
    rows_y = tall // QUARTERS
    turned = pl.pallas_call(
        deconvolve,
        out_shape=jax.ShapeDtypeStruct((tall, deep, long_x), f32),
        in_specs=[pl.BlockSpec(memory_space=pltpu.VMEM)] * 2 + [pl.BlockSpec(memory_space=pltpu.SMEM)] * 2,
        out_specs=pl.BlockSpec(memory_space=pltpu.VMEM),
        scratch_shapes=[
            pltpu.VMEM((devices, rows_y, deep, LANES), f32),
            pltpu.VMEM((2, rows_y, full_z, LANES), f32),
            pltpu.VMEM((wide, tall, full_z), f32),
            volume, volume, volume, volume,
            pltpu.VMEM((4, wide, full_y, full_z), f32),
            pltpu.VMEM((4, radius, full_y, full_z), f32),
            pltpu.VMEM((4, radius, full_y, full_z), f32),
            pltpu.VMEM((2, rows_y, full_z, LANES), f32),
            pltpu.VMEM((devices, rows_y, deep, LANES), f32),
            pltpu.VMEM((4, full_z, full_z), bf16), pltpu.VMEM((4, full_z, full_z), bf16),
            pltpu.VMEM((4, LANES, LANES), bf16), pltpu.VMEM((4, LANES, LANES), bf16),
            pltpu.SemaphoreType.DMA((devices,)), pltpu.SemaphoreType.DMA((devices,)),
            pltpu.SemaphoreType.DMA((2,)),
            pltpu.SemaphoreType.DMA((4, 2)), pltpu.SemaphoreType.DMA((4, 2)),
            pltpu.SemaphoreType.DMA((devices,)), pltpu.SemaphoreType.DMA((devices,)),
        ],
        compiler_params=pltpu.CompilerParams(
            collective_id=0, has_side_effects=True, vmem_limit_bytes=48 * 1024 * 1024
        ),
    )(view_a, view_b_own, spread_a, spread_b)
    return jnp.transpose(turned, (1, 0, 2))


def fits_slabs(mesh, view_a, view_b_own, spread_a):
    groups, sides = mesh.shape["gz"], mesh.shape["gy"]
    deep = view_a[0] // (mesh.shape["blocks"] * groups)
    tall, wide = view_a[1] // sides, view_a[2] // (2 * groups)
    return (
        sides == 2 and wide * QUARTERS == LANES and view_b_own[2] == LANES and 4 * view_a[1] == LANES
        and tall % (8 * sides) == 0 and deep % 8 == 0 and spread_a[1] % 2 == 1 and spread_a[1] // 2 <= wide // 2
    )


def solution(mesh):
    in_specs = (P(("blocks", "gz"), "gy", None), P(("blocks", "gz"), "gy", None), P(), P())
    out_specs = P(("blocks", "gz"), "gy", None)

    def run(view_a, view_b_own, spread_a, spread_b):
        plan = slab_shards if fits_slabs(mesh, view_a.shape, view_b_own.shape, spread_a.shape) else shards
        split_plan = jax.shard_map(plan, mesh=mesh, in_specs=in_specs, out_specs=out_specs, check_vma=False)
        return split_plan(view_a, view_b_own, spread_a, spread_b)

    return run
```

profile of v0, /device:TPU:1, one launch (start us, length us, event | category | flops | bytes accessed | tf_op | source)
XLA Modules:
  0.0 63.7 jit_solution(18257440986211612222)
XLA Ops:
  0.0 0.0 copy-start
  0.0 1.0 %copy-done = f32[16,16,512]{2,1,0:T(8,128)S(1)} copy-done((f32[16,16,512]{2,1,0:T(8,128)S(1)}, f32[16,16,512]{2,1,0:T(8,128)}, u32[]{:S(2)}) %copy-start) | copy-done | bytes 524312
  1.0 0.0 copy-start.1
  1.0 1.0 %copy-done.1 = f32[64,16,128]{2,1,0:T(8,128)S(1)} copy-done((f32[64,16,128]{2,1,0:T(8,128)S(1)}, f32[64,16,128]{2,1,0:T(8,128)}, u32[]{:S(2)}) %copy-start.1) | copy-done | bytes 524312
  2.1 0.0 copy-start.2
  2.1 0.7 %copy-done.2 = f32[3,31]{1,0:T(4,128)S(1)} copy-done((f32[3,31]{1,0:T(4,128)S(1)}, f32[3,31]{1,0:T(4,128)}, u32[]{:S(2)}) %copy-start.2) | copy-done | bytes 396
  2.8 0.0 copy-start.3
  2.8 0.7 %copy-done.3 = f32[3,31]{1,0:T(4,128)S(1)} copy-done((f32[3,31]{1,0:T(4,128)S(1)}, f32[3,31]{1,0:T(4,128)}, u32[]{:S(2)}) %copy-start.3) | copy-done | bytes 396
  3.4 59.2 %shard_map.46 = f32[16,16,512]{2,1,0:T(8,128)S(1)} custom-call(f32[16,16,512]{2,1,0:T(8,128)S(1)} %copy-done, f32[64,16,128]{2,1,0:T(8,128)S(1)} %copy-done.1, f32[3,31]{1,0:T(4,128)S(1)} %copy-done.2, f32[3,31]{1,0:T(4,128)S(1)} %copy-done.3), custom_call_target="tpu_custom_call" | custom-call | tf_op jit(solution)/shard_map/pallas_call | solution.py:329
  62.6 1.1 %copy.5 = f32[16,16,512]{2,1,0:T(8,128)} copy(f32[16,16,512]{2,0,1:T(8,128)S(1)} %bitcast.1) | data formatting | bytes 1048576 | tf_op jit(solution)/shard_map/transpose | solution.py:355
Async XLA Ops:
  0.0 1.0 %copy-start = (f32[16,16,512]{2,1,0:T(8,128)S(1)}, f32[16,16,512]{2,1,0:T(8,128)}, u32[]{:S(2)}) copy-start(f32[16,16,512]{2,1,0:T(8,128)} %va_ref.1) | copy-start | bytes 1572868
  1.0 1.0 %copy-start.1 = (f32[64,16,128]{2,1,0:T(8,128)S(1)}, f32[64,16,128]{2,1,0:T(8,128)}, u32[]{:S(2)}) copy-start(f32[64,16,128]{2,1,0:T(8,128)} %vb_ref.1) | copy-start | bytes 1572868
  2.1 0.7 %copy-start.2 = (f32[3,31]{1,0:T(4,128)S(1)}, f32[3,31]{1,0:T(4,128)}, u32[]{:S(2)}) copy-start(f32[3,31]{1,0:T(4,128)} %sa_ref.1) | copy-start | bytes 1120
  2.8 0.7 %copy-start.3 = (f32[3,31]{1,0:T(4,128)S(1)}, f32[3,31]{1,0:T(4,128)}, u32[]{:S(2)}) copy-start(f32[3,31]{1,0:T(4,128)} %sb_ref.1) | copy-start | bytes 1120
where the time goes:
time: 64 us; the launch traced here: 63.7 us
  Pallas kernels  59.2 us (92%)
  local copies, waits for them, and re-layouts  4.55 us (7%)
    pallas_call x1, Pallas kernels, slab_shards(): pl.pallas_call(deconvolve, out_shape=jax.ShapeDtypeStruct((tall, deep, lo...  59.2 us
    unnamed x8, local copies, waits for them, and re-layouts  3.44 us

commit v1 on v0

v1 whole, which is shorter than its diff:
```python
import functools

import jax
import jax.numpy as jnp
from jax import lax
from jax.experimental import pallas as pl
from jax.experimental.pallas import tpu as pltpu
from jax.sharding import PartitionSpec as P

LANES = 128
QUARTERS = 4
BAND = 8


def padded(cells, sides, width):
    for axis, dim in sides:
        count = lax.axis_size(axis)
        ends = count - 1
        head = lax.slice_in_dim(cells, 0, width, axis=dim)
        tail = lax.slice_in_dim(cells, cells.shape[dim] - width, cells.shape[dim], axis=dim)
        cells = jnp.concatenate(
            [
                lax.ppermute(tail, axis, [(i, (i + 1) % count) for i in range(ends)]),
                cells,
                lax.ppermute(head, axis, [((i + 1) % count, i) for i in range(ends)]),
            ],
            axis=dim,
        )
    return cells


def band_table(weights, count_in, count_out, offset):
    source = jnp.arange(count_in, dtype=jnp.int32)[:, None]
    target = jnp.arange(count_out, dtype=jnp.int32)[None, :]
    spread = source - target + offset
    table = jnp.zeros((count_in, count_out), jnp.float32)
    for place in range(weights.shape[0]):
        table = table + jnp.where(spread == place, weights[place], jnp.float32(0.0))
    return table


def blur(volume, kernels):
    count_z, count_y, count_x = volume.shape
    radius = (kernels.shape[1] - 1) // 2
    table_x = band_table(kernels[2], count_x, count_x, radius)
    along_x = jnp.einsum("zyx,xw->zyw", volume, table_x, precision=lax.Precision.HIGHEST)
    table_y = band_table(kernels[1], count_y + 2 * radius, count_y, 0)
    widened = padded(along_x, (("gy", 1),), radius)
    narrow_y = jnp.einsum("zyx,yw->zwx", widened, table_y, precision=lax.Precision.HIGHEST)
    along_y = padded(narrow_y, (("gz", 0),), radius)
    table_z = band_table(kernels[0], count_z + 2 * radius, count_z, 0)
    return jnp.einsum("zyx,zw->wyx", along_y, table_z, precision=lax.Precision.HIGHEST)


def shards(view_a, view_b_own, spread_a, spread_b):
    arrived = lax.all_to_all(view_b_own, "gz", split_axis=2, concat_axis=0, tiled=True)
    view_b = jnp.transpose(arrived, (2, 1, 0))[:, :, ::-1]
    blur_a = spread_a / jnp.sum(spread_a, axis=1, keepdims=True)
    blur_b = spread_b / jnp.sum(spread_b, axis=1, keepdims=True)
    estimate = 0.5 * (view_a + view_b)
    for measured, kernels in ((view_a, blur_a), (view_b, blur_b)):
        quotient = measured / blur(estimate, kernels)
        estimate = estimate * blur(quotient, kernels[:, ::-1])
    return estimate


def block_transpose(parts, width):
    lane = lax.broadcasted_iota(jnp.int32, parts[0].shape, 1)
    for step in (2, 1):
        shift = step * width
        low = lax.rem(lane // shift, 2) == 0
        out = list(parts)
        for first in range(QUARTERS):
            if first & step:
                continue
            second = first + step
            out[first] = jnp.where(low, parts[first], pltpu.roll(parts[second], shift, 1))
            out[second] = jnp.where(low, pltpu.roll(parts[first], LANES - shift, 1), parts[second])
        parts = out
    return parts


def split(values):
    high = values.astype(jnp.bfloat16)
    return high, (values - high.astype(jnp.float32)).astype(jnp.bfloat16)


def dot(a, b):
    return jnp.dot(a, b, preferred_element_type=jnp.float32)


def deconvolve(
    va_hbm, vb_hbm, sa_hbm, sb_hbm, out_ref,
    va_ref, vb_ref, sa_ref, sb_ref,
    send_a, recv_a, recv_b, view_a, view_b, estimate, blurred, wide_x,
    send_e, recv_e, tz_high, tz_low, ty_high, ty_low,
    in_sem, a_send_sem, a_recv_sem, b_sem, h_send_sem, h_recv_sem, e_send_sem, e_recv_sem,
):
    f32 = jnp.float32
    groups = lax.axis_size("gz")
    devices = 2 * groups
    block = lax.axis_index("blocks")
    gz, gy = lax.axis_index("gz"), lax.axis_index("gy")
    me = 2 * gz + gy
    slab = 2 * (groups - 1 - gz) + gy
    deep, tall, long_x = va_ref.shape
    wide, full_y, full_z = view_a.shape
    taps = sa_ref.shape[1]
    radius = (taps - 1) // 2
    rows_y = tall // QUARTERS
    bands = full_y // BAND
    side_bands = tall // BAND
    lines = BAND // QUARTERS
    order = [side * side_bands + half for half in range(side_bands) for side in range(2)]
    spreads = (sa_ref, sb_ref)

    def slab_of(device):
        return 2 * (groups - 1 - device // 2) + lax.rem(device, 2)

    def at(device):
        return (block, device // 2, lax.rem(device, 2))

    def device_of(place):
        return (block, groups - 1 - place // 2, lax.rem(place, 2))

    def remote(src, dst, send_sem, recv_sem, device):
        return pltpu.make_async_remote_copy(
            src_ref=src, dst_ref=dst, send_sem=send_sem, recv_sem=recv_sem,
            device_id=device, device_id_type=pl.DeviceIdType.MESH,
        )

    loads = [
        pltpu.make_async_copy(src, dst, in_sem.at[index])
        for index, (src, dst) in enumerate(
            ((va_hbm, va_ref), (vb_hbm, vb_ref), (sa_hbm, sa_ref), (sb_hbm, sb_ref))
        )
    ]
    for load in loads:
        load.start()
    barrier = pltpu.get_barrier_semaphore()
    for hop in range(1, devices):
        pl.semaphore_signal(
            barrier, inc=1, device_id=at(lax.rem(me + hop, devices)), device_id_type=pl.DeviceIdType.MESH
        )

    loads[0].wait()
    for y in range(rows_y):
        for column in range(long_x // LANES):
            pieces = [
                va_ref[:, QUARTERS * y + q, column * LANES:(column + 1) * LANES] for q in range(QUARTERS)
            ]
            for k, piece in enumerate(block_transpose(pieces, wide)):
                send_a[QUARTERS * column + k, y] = piece

    loads[1].wait()
    pl.semaphore_wait(barrier, devices - 1)

    half = remote(
        vb_ref.at[pl.ds(wide * gy, wide)], recv_b, b_sem.at[0], b_sem.at[1], (block, gz, 1 - gy)
    )
    half.start()
    own_z = pl.ds(pl.multiple_of(gz * deep, 8), deep)

    def copy_a(part, hop):
        target = lax.rem(me + hop, devices)
        rows = pl.ds(lines * part, lines)
        return remote(
            send_a.at[slab_of(target), rows], recv_a.at[gy, rows, own_z],
            a_send_sem.at[part, hop], a_recv_sem.at[part, hop], at(target),
        )

    for part in range(side_bands):
        for hop in range(1, devices):
            copy_a(part, hop).start()
    recv_a[gy, :, own_z] = send_a[slab]

    loads[2].wait()
    loads[3].wait()
    row = lax.broadcasted_iota(jnp.int32, (full_z, LANES), 0)
    col = lax.broadcasted_iota(jnp.int32, (full_z, LANES), 1)
    for which, spread in enumerate(spreads):
        total = f32(1.0)
        for axis in range(3):
            line = spread[axis, 0]
            for tap in range(1, taps):
                line = line + spread[axis, tap]
            total = total * line
        for flipped in range(2):
            index = 2 * which + flipped
            sign = -1 if flipped else 1
            offset = sign * (row - col) + radius
            table = jnp.zeros((full_z, LANES), f32)
            for tap in range(taps):
                table = jnp.where(offset == tap, spread[0, tap], table)
            table = table / jnp.full((full_z, LANES), total, f32)
            tz_high[index], tz_low[index] = split(table)
            offset = jnp.where(row // full_y == col // full_y, sign * (col - row) + radius, -1)
            table = jnp.zeros((LANES, LANES), f32)
            for tap in range(taps):
                table = jnp.where(offset == tap, spread[1, tap], table)
            ty_high[index], ty_low[index] = split(table)

    mine, other = pl.multiple_of(gy * tall, 8), pl.multiple_of((1 - gy) * tall, 8)
    for x in range(wide):
        view_b[x, pl.ds(mine, tall)] = vb_ref[2 * wide - 1 - wide * gy - x]
    half.wait()
    for x in range(wide):
        view_b[x, pl.ds(other, tall)] = recv_b[wide - 1 - x]

    outer = jnp.where(gy == 0, slab > 0, slab < devices - 1)
    neighbour = device_of(jnp.clip(slab + 2 * gy - 1, 0, devices - 1))

    @pl.when(jnp.logical_not(outer))
    def _():
        for turn in range(4):
            wide_x[turn, pl.ds((radius + wide) * gy, radius)] = jnp.zeros((radius, full_y, full_z), f32)

    def halo(turn, band, inner):
        ys = pl.ds(band * BAND, BAND) if isinstance(band, int) else pl.ds(pl.multiple_of(band * BAND, BAND), BAND)
        source = radius + (wide - radius) * ((1 - gy) if inner else gy)
        target = (radius + wide) * (gy if inner else (1 - gy))
        return remote(
            wide_x.at[turn, pl.ds(source, radius), ys], wide_x.at[turn, pl.ds(target, radius), ys],
            h_send_sem.at[turn, band, inner], h_recv_sem.at[turn, band, inner],
            (block, gz, 1 - gy) if inner else neighbour,
        )

    def send_outer(turn, band):
        pl.when(outer)(halo(turn, band, 0).start)

    def send_inner(turn, band):
        halo(turn, band, 1).start()

    def await_halos(turn, band):
        halo(turn, band, 1).wait_recv()
        pl.when(outer)(halo(turn, band, 0).wait_recv)

    def x_taps(turn, which, flipped, band, edges, finish):
        ys = pl.ds(band * BAND, BAND) if isinstance(band, int) else pl.ds(pl.multiple_of(band * BAND, BAND), BAND)
        spread = spreads[which]
        weights = [spread[2, taps - 1 - tap if flipped else tap] for tap in range(taps)]
        for x in range(wide):
            total = blurred[x, ys] if edges else None
            for tap in range(taps):
                place = x + tap
                if (radius <= place < radius + wide) != edges:
                    term = weights[tap] * wide_x[turn, place, ys]
                    total = term if total is None else total + term
            finish(x, ys, total)

    def keep(x, ys, total):
        blurred[x, ys] = total

    for part in range(side_bands):
        for hop in range(1, devices):
            copy_a(part, hop).wait_recv()
        for side in range(2):
            for y in range(lines * part, lines * (part + 1)):
                turned = recv_a[side, y].T
                for q in range(QUARTERS):
                    view_a[:, side * tall + QUARTERS * y + q, :] = turned[q * wide:(q + 1) * wide]
        for side in range(2):
            band = side * side_bands + part
            ys = pl.ds(band * BAND, BAND)
            start = 0.5 * (view_a[:, ys] + view_b[:, ys])
            estimate[:, ys] = start
            wide_x[0, pl.ds(radius, wide), ys] = start
            send_outer(0, band)
            send_inner(0, band)

    planes = LANES // full_y
    chunks = wide // planes // 2

    def along_zy(values, index):
        high, low = split(values.reshape(chunks * LANES, full_z))
        zh = tz_high[index]
        done = dot(high, zh) + (dot(low, zh) + dot(high, tz_low[index]))
        high, low = split(done)
        yh, yl = ty_high[index], ty_low[index]
        outs = []
        for chunk in range(chunks):
            rows = slice(chunk * LANES, (chunk + 1) * LANES)
            outs.append(dot(yh, high[rows]) + (dot(yh, low[rows]) + dot(yl, high[rows])))
        return jnp.concatenate(outs, axis=0).reshape(wide // 2, full_y, full_z)

    def middle(turn, which, view):
        for step in range(2):
            first = (wide // 2) * (gy if step == 0 else 1 - gy)
            span = pl.ds(first, wide // 2)
            quotient = view[span] / along_zy(blurred[span], 2 * which)
            wide_x[turn, pl.ds(radius + first, wide // 2)] = along_zy(quotient, 2 * which + 1)
            for band in order:
                (send_inner if step else send_outer)(turn, band)

    def looped(body):
        def step(index, carry):
            body(lax.rem(index, 2) * side_bands + index // 2)
            return carry

        lax.fori_loop(0, bands, step, 0)

    looped(lambda band: x_taps(0, 0, 0, band, False, keep))

    def first_edges(band):
        await_halos(0, band)
        x_taps(0, 0, 0, band, True, keep)

    looped(first_edges)
    middle(1, 0, view_a)
    looped(lambda band: x_taps(1, 0, 1, band, False, keep))

    def update(x, ys, total):
        value = estimate[x, ys] * total
        estimate[x, ys] = value
        wide_x[2, radius + x, ys] = value

    def second_edges(band):
        await_halos(1, band)
        x_taps(1, 0, 1, band, True, update)
        send_outer(2, band)
        send_inner(2, band)
        x_taps(2, 1, 0, band, False, keep)

    looped(second_edges)

    def third_edges(band):
        await_halos(2, band)
        x_taps(2, 1, 0, band, True, keep)

    looped(third_edges)
    middle(3, 1, view_b)
    looped(lambda band: x_taps(3, 1, 1, band, False, keep))

    def last(x, ys, total):
        estimate[x, ys] = estimate[x, ys] * total

    def copy_e(side, part, step):
        target = 2 * lax.rem(gz + step, groups) + side
        hop = lax.rem(target - me + devices, devices)
        rows = pl.ds(lines * part, lines)
        return remote(
            send_e.at[side, rows, pl.ds(pl.multiple_of(target // 2 * deep, 8), deep)], recv_e.at[slab, rows],
            e_send_sem.at[part, hop], e_recv_sem.at[part, hop], at(target),
        )

    for band in order:
        side, part = band // side_bands, band % side_bands
        await_halos(3, band)
        x_taps(3, 1, 1, band, True, last)
        for y in range(lines * part, lines * (part + 1)):
            strips = [estimate[:, side * tall + QUARTERS * y + q, :] for q in range(QUARTERS)]
            send_e[side, y] = jnp.concatenate(strips, axis=0).T
        for step in range(1, groups):
            copy_e(side, part, step).start()
        pl.when(gy != side)(copy_e(side, part, 0).start)

    recv_e[slab] = send_e[gy, :, own_z]
    for part in range(side_bands):
        for hop in range(1, devices):
            remote(
                send_e.at[0, pl.ds(0, lines), pl.ds(0, deep)], recv_e.at[slab, pl.ds(lines * part, lines)],
                e_send_sem.at[part, hop], e_recv_sem.at[part, hop], at(lax.rem(me + hop, devices)),
            ).wait_recv()
        for y in range(lines * part, lines * (part + 1)):
            for column in range(long_x // LANES):
                pieces = [recv_e[QUARTERS * column + k, y] for k in range(QUARTERS)]
                for q, piece in enumerate(block_transpose(pieces, wide)):
                    out_ref[QUARTERS * y + q, :, column * LANES:(column + 1) * LANES] = piece

    for part in range(side_bands):
        for hop in range(1, devices):
            copy_a(part, hop).wait_send()
        for side in range(2):
            for step in range(1, groups):
                copy_e(side, part, step).wait_send()
            pl.when(gy != side)(copy_e(side, part, 0).wait_send)
    for turn in range(4):
        for band in range(bands):
            halo(turn, band, 1).wait_send()
            pl.when(outer)(halo(turn, band, 0).wait_send)


def slab_shards(view_a, view_b_own, spread_a, spread_b):
    groups = lax.axis_size("gz")
    deep, tall, long_x = view_a.shape
    devices = 2 * groups
    wide = long_x // devices
    full_y, full_z = 2 * tall, view_b_own.shape[2]
    taps = spread_a.shape[1]
    radius = (taps - 1) // 2
    f32, bf16 = jnp.float32, jnp.bfloat16
    volume = pltpu.VMEM((wide, full_y, full_z), f32)
    rows_y = tall // QUARTERS
    bands, halves = full_y // BAND, tall // BAND
    dma = pltpu.SemaphoreType.DMA
    turned = pl.pallas_call(
        deconvolve,
        out_shape=jax.ShapeDtypeStruct((tall, deep, long_x), f32),
        in_specs=[pl.BlockSpec(memory_space=pl.ANY)] * 4,
        out_specs=pl.BlockSpec(memory_space=pltpu.VMEM),
        scratch_shapes=[
            pltpu.VMEM(view_a.shape, f32), pltpu.VMEM(view_b_own.shape, f32),
            pltpu.SMEM(spread_a.shape, f32), pltpu.SMEM(spread_b.shape, f32),
            pltpu.VMEM((devices, rows_y, deep, LANES), f32),
            pltpu.VMEM((2, rows_y, full_z, LANES), f32),
            pltpu.VMEM((wide, tall, full_z), f32),
            volume, volume, volume, volume,
            pltpu.VMEM((4, wide + 2 * radius, full_y, full_z), f32),
            pltpu.VMEM((2, rows_y, full_z, LANES), f32),
            pltpu.VMEM((devices, rows_y, deep, LANES), f32),
            pltpu.VMEM((4, full_z, full_z), bf16), pltpu.VMEM((4, full_z, full_z), bf16),
            pltpu.VMEM((4, LANES, LANES), bf16), pltpu.VMEM((4, LANES, LANES), bf16),
            dma((4,)), dma((halves, devices)), dma((halves, devices)), dma((2,)),
            dma((4, bands, 2)), dma((4, bands, 2)), dma((halves, devices)), dma((halves, devices)),
        ],
        compiler_params=pltpu.CompilerParams(
            collective_id=0, has_side_effects=True, vmem_limit_bytes=48 * 1024 * 1024
        ),
    )(view_a, view_b_own, spread_a, spread_b)
    return jnp.transpose(turned, (1, 0, 2))


def fits_slabs(mesh, view_a, view_b_own, spread_a):
    groups, sides = mesh.shape["gz"], mesh.shape["gy"]
    deep = view_a[0] // (mesh.shape["blocks"] * groups)
    tall, wide = view_a[1] // sides, view_a[2] // (2 * groups)
    return (
        sides == 2 and wide * QUARTERS == LANES and view_b_own[2] == LANES and 4 * view_a[1] == LANES
        and tall % (8 * sides) == 0 and deep % 8 == 0 and spread_a[1] % 2 == 1 and spread_a[1] // 2 <= wide // 2
    )


def solution(mesh):
    in_specs = (P(("blocks", "gz"), "gy", None), P(("blocks", "gz"), "gy", None), P(), P())
    out_specs = P(("blocks", "gz"), "gy", None)

    def run(view_a, view_b_own, spread_a, spread_b):
        plan = slab_shards if fits_slabs(mesh, view_a.shape, view_b_own.shape, spread_a.shape) else shards
        split_plan = jax.shard_map(plan, mesh=mesh, in_specs=in_specs, out_specs=out_specs, check_vma=False)
        return split_plan(view_a, view_b_own, spread_a, spread_b)

    return run
```

time: 64 us -> 60.1 us (0.939)
  Pallas kernels: 59.2 us -> 55.3 us
    pallas_call x1, Pallas kernels: 59.2 us -> 55.3 us  [slab_shards(): pl.pallas_call(deconvolve, out_shape=jax.ShapeDtypeStruct((tall, deep, lo...]
where the time goes in v1:
time: 60.1 us; the launch traced here: 59.9 us
  Pallas kernels  55.3 us (92%)
  local copies, waits for them, and re-layouts  4.55 us (8%)
    pallas_call x1, Pallas kernels, slab_shards(): pl.pallas_call(deconvolve, out_shape=jax.ShapeDtypeStruct((tall, deep, lo...  55.3 us
    unnamed x8, local copies, waits for them, and re-layouts  3.44 us

profile of v1, /device:TPU:1, one launch (start us, length us, event | category | flops | bytes accessed | tf_op | source)
XLA Modules:
  0.0 59.9 jit_solution(9770924864397183640)
XLA Ops:
  0.0 0.0 copy-start
  0.0 1.0 %copy-done = f32[16,16,512]{2,1,0:T(8,128)S(1)} copy-done((f32[16,16,512]{2,1,0:T(8,128)S(1)}, f32[16,16,512]{2,1,0:T(8,128)}, u32[]{:S(2)}) %copy-start) | copy-done | bytes 524312
  1.0 0.0 copy-start.1
  1.0 1.0 %copy-done.1 = f32[64,16,128]{2,1,0:T(8,128)S(1)} copy-done((f32[64,16,128]{2,1,0:T(8,128)S(1)}, f32[64,16,128]{2,1,0:T(8,128)}, u32[]{:S(2)}) %copy-start.1) | copy-done | bytes 524312
  2.1 0.0 copy-start.2
  2.1 0.7 %copy-done.2 = f32[3,31]{1,0:T(4,128)S(1)} copy-done((f32[3,31]{1,0:T(4,128)S(1)}, f32[3,31]{1,0:T(4,128)}, u32[]{:S(2)}) %copy-start.2) | copy-done | bytes 396
  2.8 0.0 copy-start.3
  2.8 0.7 %copy-done.3 = f32[3,31]{1,0:T(4,128)S(1)} copy-done((f32[3,31]{1,0:T(4,128)S(1)}, f32[3,31]{1,0:T(4,128)}, u32[]{:S(2)}) %copy-start.3) | copy-done | bytes 396
  3.4 55.3 %shard_map.46 = f32[16,16,512]{2,1,0:T(8,128)S(1)} custom-call(f32[16,16,512]{2,1,0:T(8,128)S(1)} %copy-done, f32[64,16,128]{2,1,0:T(8,128)S(1)} %copy-done.1, f32[3,31]{1,0:T(4,128)S(1)} %copy-done.2, f32[3,31]{1,0:T(4,128)S(1)} %copy-done.3), custom_call_target="tpu_custom_call" | custom-call | tf_op jit(solution)/shard_map/pallas_call | solution.py:396
  58.8 1.1 %copy.5 = f32[16,16,512]{2,1,0:T(8,128)} copy(f32[16,16,512]{2,0,1:T(8,128)S(1)} %bitcast.1) | data formatting | bytes 1048576 | tf_op jit(solution)/shard_map/transpose | solution.py:420
Async XLA Ops:
  0.0 1.0 %copy-start = (f32[16,16,512]{2,1,0:T(8,128)S(1)}, f32[16,16,512]{2,1,0:T(8,128)}, u32[]{:S(2)}) copy-start(f32[16,16,512]{2,1,0:T(8,128)} %va_hbm.1) | copy-start | bytes 1572868
  1.0 1.0 %copy-start.1 = (f32[64,16,128]{2,1,0:T(8,128)S(1)}, f32[64,16,128]{2,1,0:T(8,128)}, u32[]{:S(2)}) copy-start(f32[64,16,128]{2,1,0:T(8,128)} %vb_hbm.1) | copy-start | bytes 1572868
  2.1 0.7 %copy-start.2 = (f32[3,31]{1,0:T(4,128)S(1)}, f32[3,31]{1,0:T(4,128)}, u32[]{:S(2)}) copy-start(f32[3,31]{1,0:T(4,128)} %sa_hbm.1) | copy-start | bytes 1120
  2.8 0.7 %copy-start.3 = (f32[3,31]{1,0:T(4,128)S(1)}, f32[3,31]{1,0:T(4,128)}, u32[]{:S(2)}) copy-start(f32[3,31]{1,0:T(4,128)} %sb_hbm.1) | copy-start | bytes 1120

commit v2 on v1

--- a/solution.py
+++ b/solution.py
@@ -92,9 +92,9 @@
 def deconvolve(
     va_hbm, vb_hbm, sa_hbm, sb_hbm, out_ref,
     va_ref, vb_ref, sa_ref, sb_ref,
-    send_a, recv_a, recv_b, view_a, view_b, estimate, blurred, wide_x,
+    send_a, recv_a, recv_b, relay, view_a, view_b, estimate, blurred, wide_x,
     send_e, recv_e, tz_high, tz_low, ty_high, ty_low,
-    in_sem, a_send_sem, a_recv_sem, b_sem, h_send_sem, h_recv_sem, e_send_sem, e_recv_sem,
+    in_sem, a_send_sem, a_recv_sem, b_send_sem, b_recv_sem, r_send_sem, r_recv_sem, h_send_sem, h_recv_sem, e_send_sem, e_recv_sem,
 ):
     f32 = jnp.float32
     groups = lax.axis_size("gz")
@@ -102,7 +102,6 @@
     block = lax.axis_index("blocks")
     gz, gy = lax.axis_index("gz"), lax.axis_index("gy")
     me = 2 * gz + gy
-    slab = 2 * (groups - 1 - gz) + gy
     deep, tall, long_x = va_ref.shape
     wide, full_y, full_z = view_a.shape
     taps = sa_ref.shape[1]
@@ -113,15 +112,23 @@
     lines = BAND // QUARTERS
     order = [side * side_bands + half for half in range(side_bands) for side in range(2)]
     spreads = (sa_ref, sb_ref)
+    mirror = gz + 1 - 2 * lax.rem(gz, 2)
+    crossed = lax.rem(gz // 2 + block, 2) == 1
+    direct_x = wide // 2
+
+    def snake(group):
+        return jnp.where(lax.rem(group // 2 + block, 2) == 1, group + 1 - 2 * lax.rem(group, 2), group)
 
     def slab_of(device):
-        return 2 * (groups - 1 - device // 2) + lax.rem(device, 2)
+        return 2 * (groups - 1 - snake(device // 2)) + lax.rem(device, 2)
 
     def at(device):
         return (block, device // 2, lax.rem(device, 2))
 
     def device_of(place):
-        return (block, groups - 1 - place // 2, lax.rem(place, 2))
+        return (block, snake(groups - 1 - place // 2), lax.rem(place, 2))
+
+    slab = slab_of(me)
 
     def remote(src, dst, send_sem, recv_sem, device):
         return pltpu.make_async_remote_copy(
@@ -141,6 +148,11 @@
     for hop in range(1, devices):
         pl.semaphore_signal(
             barrier, inc=1, device_id=at(lax.rem(me + hop, devices)), device_id_type=pl.DeviceIdType.MESH
+        )
+
+    for group, core in ((gz, gy), (mirror, 0), (mirror, 1)):
+        pl.semaphore_signal(
+            barrier, inc=1, device_id=(1 - block, group, core), device_id_type=pl.DeviceIdType.MESH
         )
 
     loads[0].wait()
@@ -153,12 +165,36 @@
                 send_a[QUARTERS * column + k, y] = piece
 
     loads[1].wait()
-    pl.semaphore_wait(barrier, devices - 1)
+    pl.semaphore_wait(barrier, devices + 2)
 
     half = remote(
-        vb_ref.at[pl.ds(wide * gy, wide)], recv_b, b_sem.at[0], b_sem.at[1], (block, gz, 1 - gy)
+        vb_ref.at[pl.ds(wide * gy, wide)], recv_b.at[gy], b_send_sem.at[0, 0], b_recv_sem.at[gy, 0], (block, gz, 1 - gy)
     )
-    half.start()
+
+    def direct(core):
+        return remote(
+            vb_ref.at[pl.ds(wide * (1 - core), direct_x)], recv_b.at[gy, pl.ds(0, direct_x)],
+            b_send_sem.at[core, 0], b_recv_sem.at[gy, 0], (block, mirror, core),
+        )
+
+    def detour(core):
+        return remote(
+            vb_ref.at[pl.ds(wide * (1 - core) + direct_x, wide - direct_x)], relay.at[core],
+            b_send_sem.at[core, 1], r_recv_sem.at[core], (1 - block, gz, gy),
+        )
+
+    def onward(core):
+        return remote(
+            relay.at[core], recv_b.at[gy, pl.ds(direct_x, wide - direct_x)],
+            r_send_sem.at[core], b_recv_sem.at[gy, 1], (1 - block, mirror, core),
+        )
+
+    @pl.when(crossed)
+    def _():
+        for core in range(2):
+            detour(core).start()
+
+    pl.when(jnp.logical_not(crossed))(half.start)
     own_z = pl.ds(pl.multiple_of(gz * deep, 8), deep)
 
     def copy_a(part, hop):
@@ -173,6 +209,12 @@
         for hop in range(1, devices):
             copy_a(part, hop).start()
     recv_a[gy, :, own_z] = send_a[slab]
+
+    @pl.when(crossed)
+    def _():
+        for core in range(2):
+            direct(core).start()
+
 
     loads[2].wait()
     loads[3].wait()
@@ -201,11 +243,34 @@
             ty_high[index], ty_low[index] = split(table)
 
     mine, other = pl.multiple_of(gy * tall, 8), pl.multiple_of((1 - gy) * tall, 8)
+
+    @pl.when(jnp.logical_not(crossed))
+    def _():
+        for core in range(2):
+            detour(core).wait_recv()
+            onward(core).start()
+        for x in range(wide):
+            view_b[x, pl.ds(mine, tall)] = vb_ref[2 * wide - 1 - wide * gy - x]
+        remote(
+            vb_ref.at[pl.ds(0, wide)], recv_b.at[0], b_send_sem.at[0, 0], b_recv_sem.at[1 - gy, 0], (block, gz, 1 - gy)
+        ).wait_recv()
+
+    @pl.when(crossed)
+    def _():
+        for core in range(2):
+            remote(
+                vb_ref.at[pl.ds(0, direct_x)], recv_b.at[core, pl.ds(0, direct_x)],
+                b_send_sem.at[0, 0], b_recv_sem.at[core, 0], (block, mirror, core),
+            ).wait_recv()
+            remote(
+                relay.at[0], recv_b.at[core, pl.ds(direct_x, wide - direct_x)],
+                r_send_sem.at[0], b_recv_sem.at[core, 1], (1 - block, mirror, core),
+            ).wait_recv()
+        for x in range(wide):
+            view_b[x, pl.ds(mine, tall)] = recv_b[gy, wide - 1 - x]
+
     for x in range(wide):
-        view_b[x, pl.ds(mine, tall)] = vb_ref[2 * wide - 1 - wide * gy - x]
-    half.wait()
-    for x in range(wide):
-        view_b[x, pl.ds(other, tall)] = recv_b[wide - 1 - x]
+        view_b[x, pl.ds(other, tall)] = recv_b[1 - gy, wide - 1 - x]
 
     outer = jnp.where(gy == 0, slab > 0, slab < devices - 1)
     neighbour = device_of(jnp.clip(slab + 2 * gy - 1, 0, devices - 1))
@@ -374,6 +439,19 @@
             for step in range(1, groups):
                 copy_e(side, part, step).wait_send()
             pl.when(gy != side)(copy_e(side, part, 0).wait_send)
+
+    @pl.when(crossed)
+    def _():
+        for core in range(2):
+            detour(core).wait_send()
+            direct(core).wait_send()
+
+    @pl.when(jnp.logical_not(crossed))
+    def _():
+        half.wait_send()
+        for core in range(2):
+            onward(core).wait_send()
+
     for turn in range(4):
         for band in range(bands):
             halo(turn, band, 1).wait_send()
@@ -403,18 +481,19 @@
             pltpu.SMEM(spread_a.shape, f32), pltpu.SMEM(spread_b.shape, f32),
             pltpu.VMEM((devices, rows_y, deep, LANES), f32),
             pltpu.VMEM((2, rows_y, full_z, LANES), f32),
-            pltpu.VMEM((wide, tall, full_z), f32),
+            pltpu.VMEM((2, wide, tall, full_z), f32),
+            pltpu.VMEM((2, wide // 2, tall, full_z), f32),
             volume, volume, volume, volume,
             pltpu.VMEM((4, wide + 2 * radius, full_y, full_z), f32),
             pltpu.VMEM((2, rows_y, full_z, LANES), f32),
             pltpu.VMEM((devices, rows_y, deep, LANES), f32),
             pltpu.VMEM((4, full_z, full_z), bf16), pltpu.VMEM((4, full_z, full_z), bf16),
             pltpu.VMEM((4, LANES, LANES), bf16), pltpu.VMEM((4, LANES, LANES), bf16),
-            dma((4,)), dma((halves, devices)), dma((halves, devices)), dma((2,)),
+            dma((4,)), dma((halves, devices)), dma((halves, devices)), dma((2, 2)), dma((2, 2)), dma((2,)), dma((2,)),
             dma((4, bands, 2)), dma((4, bands, 2)), dma((halves, devices)), dma((halves, devices)),
         ],
         compiler_params=pltpu.CompilerParams(
-            collective_id=0, has_side_effects=True, vmem_limit_bytes=48 * 1024 * 1024
+            collective_id=0, has_side_effects=True, vmem_limit_bytes=56000000
         ),
     )(view_a, view_b_own, spread_a, spread_b)
     return jnp.transpose(turned, (1, 0, 2))
@@ -425,7 +504,7 @@
     deep = view_a[0] // (mesh.shape["blocks"] * groups)
     tall, wide = view_a[1] // sides, view_a[2] // (2 * groups)
     return (
-        sides == 2 and wide * QUARTERS == LANES and view_b_own[2] == LANES and 4 * view_a[1] == LANES
+        mesh.shape["blocks"] == 2 and groups % 2 == 0 and sides == 2 and wide * QUARTERS == LANES and view_b_own[2] == LANES and 4 * view_a[1] == LANES
         and tall % (8 * sides) == 0 and deep % 8 == 0 and spread_a[1] % 2 == 1 and spread_a[1] // 2 <= wide // 2
     )
 

time: 60.1 us -> 55.5 us (0.923)
  Pallas kernels: 55.3 us -> 52.8 us
  local copies, waits for them, and re-layouts: 4.55 us -> 2.46 us
    pallas_call x1, Pallas kernels: 55.3 us -> 52.8 us  [slab_shards(): pl.pallas_call(deconvolve, out_shape=jax.ShapeDtypeStruct((tall, deep, lo...]
    unnamed x8 -> x4, local copies, waits for them, and re-layouts: 3.44 us -> 1.36 us
where the time goes in v2:
time: 55.5 us; the launch traced here: 55.3 us
  Pallas kernels  52.8 us (95%)
  local copies, waits for them, and re-layouts  2.46 us (4%)
    pallas_call x1, Pallas kernels, slab_shards(): pl.pallas_call(deconvolve, out_shape=jax.ShapeDtypeStruct((tall, deep, lo...  52.8 us
    unnamed x4, local copies, waits for them, and re-layouts  1.36 us

profile of v2, /device:TPU:1, one launch (start us, length us, event | category | flops | bytes accessed | tf_op | source)
XLA Modules:
  0.0 55.3 jit_solution(4105644962482040371)
XLA Ops:
  0.0 0.0 copy-start
  0.0 0.7 %copy-done = f32[3,31]{1,0:T(4,128)S(1)} copy-done((f32[3,31]{1,0:T(4,128)S(1)}, f32[3,31]{1,0:T(4,128)}, u32[]{:S(2)}) %copy-start) | copy-done | bytes 396
  0.7 0.0 copy-start.1
  0.7 0.7 %copy-done.1 = f32[3,31]{1,0:T(4,128)S(1)} copy-done((f32[3,31]{1,0:T(4,128)S(1)}, f32[3,31]{1,0:T(4,128)}, u32[]{:S(2)}) %copy-start.1) | copy-done | bytes 396
  1.4 52.8 %shard_map.46 = f32[16,16,512]{2,1,0:T(8,128)S(1)} custom-call(f32[16,16,512]{2,1,0:T(8,128)} %va_hbm.1, f32[64,16,128]{2,1,0:T(8,128)} %vb_hbm.1, f32[3,31]{1,0:T(4,128)S(1)} %copy-done, f32[3,31]{1,0:T(4,128)S(1)} %copy-done.1), custom_call_target="tpu_custom_call" | custom-call | tf_op jit(solution)/shard_map/pallas_call | solution.py:474
  54.2 1.1 %copy.5 = f32[16,16,512]{2,1,0:T(8,128)} copy(f32[16,16,512]{2,0,1:T(8,128)S(1)} %bitcast.1) | data formatting | bytes 1048576 | tf_op jit(solution)/shard_map/transpose | solution.py:499
Async XLA Ops:
  0.0 0.7 %copy-start = (f32[3,31]{1,0:T(4,128)S(1)}, f32[3,31]{1,0:T(4,128)}, u32[]{:S(2)}) copy-start(f32[3,31]{1,0:T(4,128)} %sa_hbm.1) | copy-start | bytes 1120
  0.7 0.7 %copy-start.1 = (f32[3,31]{1,0:T(4,128)S(1)}, f32[3,31]{1,0:T(4,128)}, u32[]{:S(2)}) copy-start(f32[3,31]{1,0:T(4,128)} %sb_hbm.1) | copy-start | bytes 1120

commit v3 on v2

--- a/solution.py
+++ b/solution.py
@@ -93,7 +93,7 @@
     va_hbm, vb_hbm, sa_hbm, sb_hbm, out_ref,
     va_ref, vb_ref, sa_ref, sb_ref,
     send_a, recv_a, recv_b, relay, view_a, view_b, estimate, blurred, wide_x,
-    send_e, recv_e, tz_high, tz_low, ty_high, ty_low,
+    send_e, recv_e, table_z, table_y,
     in_sem, a_send_sem, a_recv_sem, b_send_sem, b_recv_sem, r_send_sem, r_recv_sem, h_send_sem, h_recv_sem, e_send_sem, e_recv_sem,
 ):
     f32 = jnp.float32
@@ -136,6 +136,17 @@
             device_id=device, device_id_type=pl.DeviceIdType.MESH,
         )
 
+    barrier = pltpu.get_barrier_semaphore()
+    for hop in range(1, devices):
+        pl.semaphore_signal(
+            barrier, inc=1, device_id=at(lax.rem(me + hop, devices)), device_id_type=pl.DeviceIdType.MESH
+        )
+
+    for group, core in ((gz, gy), (mirror, 0), (mirror, 1)):
+        pl.semaphore_signal(
+            barrier, inc=1, device_id=(1 - block, group, core), device_id_type=pl.DeviceIdType.MESH
+        )
+
     loads = [
         pltpu.make_async_copy(src, dst, in_sem.at[index])
         for index, (src, dst) in enumerate(
@@ -144,17 +155,6 @@
     ]
     for load in loads:
         load.start()
-    barrier = pltpu.get_barrier_semaphore()
-    for hop in range(1, devices):
-        pl.semaphore_signal(
-            barrier, inc=1, device_id=at(lax.rem(me + hop, devices)), device_id_type=pl.DeviceIdType.MESH
-        )
-
-    for group, core in ((gz, gy), (mirror, 0), (mirror, 1)):
-        pl.semaphore_signal(
-            barrier, inc=1, device_id=(1 - block, group, core), device_id_type=pl.DeviceIdType.MESH
-        )
-
     loads[0].wait()
     for y in range(rows_y):
         for column in range(long_x // LANES):
@@ -168,31 +168,35 @@
     pl.semaphore_wait(barrier, devices + 2)
 
     half = remote(
-        vb_ref.at[pl.ds(wide * gy, wide)], recv_b.at[gy], b_send_sem.at[0, 0], b_recv_sem.at[gy, 0], (block, gz, 1 - gy)
+        vb_ref.at[pl.ds(wide * gy, wide)], recv_b.at[gy], b_send_sem.at[0, 0, 0], b_recv_sem.at[gy, 0, 0], (block, gz, 1 - gy)
     )
 
-    def direct(core):
+    def direct(core, part):
+        ys = pl.ds(BAND * part, BAND)
         return remote(
-            vb_ref.at[pl.ds(wide * (1 - core), direct_x)], recv_b.at[gy, pl.ds(0, direct_x)],
-            b_send_sem.at[core, 0], b_recv_sem.at[gy, 0], (block, mirror, core),
-        )
-
-    def detour(core):
+            vb_ref.at[pl.ds(wide * (1 - core), direct_x), ys], recv_b.at[gy, pl.ds(0, direct_x), ys],
+            b_send_sem.at[core, 0, part], b_recv_sem.at[gy, 0, part], (block, mirror, core),
+        )
+
+    def detour(core, part):
+        ys = pl.ds(BAND * part, BAND)
         return remote(
-            vb_ref.at[pl.ds(wide * (1 - core) + direct_x, wide - direct_x)], relay.at[core],
-            b_send_sem.at[core, 1], r_recv_sem.at[core], (1 - block, gz, gy),
-        )
-
-    def onward(core):
+            vb_ref.at[pl.ds(wide * (1 - core) + direct_x, wide - direct_x), ys], relay.at[core, part],
+            b_send_sem.at[core, 1, part], r_recv_sem.at[core, part], (1 - block, gz, gy),
+        )
+
+    def onward(core, part):
+        ys = pl.ds(BAND * part, BAND)
         return remote(
-            relay.at[core], recv_b.at[gy, pl.ds(direct_x, wide - direct_x)],
-            r_send_sem.at[core], b_recv_sem.at[gy, 1], (1 - block, mirror, core),
+            relay.at[core, part], recv_b.at[gy, pl.ds(direct_x, wide - direct_x), ys],
+            r_send_sem.at[core, part], b_recv_sem.at[gy, 1, part], (1 - block, mirror, core),
         )
 
     @pl.when(crossed)
     def _():
-        for core in range(2):
-            detour(core).start()
+        for part in range(side_bands):
+            for core in range(2):
+                detour(core, part).start()
 
     pl.when(jnp.logical_not(crossed))(half.start)
     own_z = pl.ds(pl.multiple_of(gz * deep, 8), deep)
@@ -208,13 +212,13 @@
     for part in range(side_bands):
         for hop in range(1, devices):
             copy_a(part, hop).start()
+
+        @pl.when(crossed)
+        def _():
+            for core in range(2):
+                direct(core, part).start()
+
     recv_a[gy, :, own_z] = send_a[slab]
-
-    @pl.when(crossed)
-    def _():
-        for core in range(2):
-            direct(core).start()
-
 
     loads[2].wait()
     loads[3].wait()
@@ -235,42 +239,52 @@
             for tap in range(taps):
                 table = jnp.where(offset == tap, spread[0, tap], table)
             table = table / jnp.full((full_z, LANES), total, f32)
-            tz_high[index], tz_low[index] = split(table)
+            high, low = split(table)
+            blank = jnp.zeros((full_z, LANES), jnp.bfloat16)
+            table_z[index] = jnp.concatenate(
+                [jnp.concatenate([high, low], axis=1), jnp.concatenate([high, blank], axis=1)], axis=0
+            )
             offset = jnp.where(row // full_y == col // full_y, sign * (col - row) + radius, -1)
             table = jnp.zeros((LANES, LANES), f32)
             for tap in range(taps):
                 table = jnp.where(offset == tap, spread[1, tap], table)
-            ty_high[index], ty_low[index] = split(table)
-
-    mine, other = pl.multiple_of(gy * tall, 8), pl.multiple_of((1 - gy) * tall, 8)
+            high, low = split(table)
+            blank = jnp.zeros((LANES, LANES), jnp.bfloat16)
+            table_y[index] = jnp.concatenate(
+                [jnp.concatenate([high, high], axis=1), jnp.concatenate([low, blank], axis=1)], axis=0
+            )
+
+    mine = pl.multiple_of(gy * tall, BAND)
 
     @pl.when(jnp.logical_not(crossed))
     def _():
-        for core in range(2):
-            detour(core).wait_recv()
-            onward(core).start()
+        for part in range(side_bands):
+            for core in range(2):
+                detour(core, part).wait_recv()
+                onward(core, part).start()
         for x in range(wide):
             view_b[x, pl.ds(mine, tall)] = vb_ref[2 * wide - 1 - wide * gy - x]
         remote(
-            vb_ref.at[pl.ds(0, wide)], recv_b.at[0], b_send_sem.at[0, 0], b_recv_sem.at[1 - gy, 0], (block, gz, 1 - gy)
+            vb_ref.at[pl.ds(0, wide)], recv_b.at[0], b_send_sem.at[0, 0, 0], b_recv_sem.at[1 - gy, 0, 0],
+            (block, gz, 1 - gy),
         ).wait_recv()
-
-    @pl.when(crossed)
-    def _():
+        other = pl.multiple_of((1 - gy) * tall, BAND)
+        for x in range(wide):
+            view_b[x, pl.ds(other, tall)] = recv_b[1 - gy, wide - 1 - x]
+
+    def crossed_view(part):
         for core in range(2):
+            ys = pl.ds(BAND * part, BAND)
             remote(
-                vb_ref.at[pl.ds(0, direct_x)], recv_b.at[core, pl.ds(0, direct_x)],
-                b_send_sem.at[0, 0], b_recv_sem.at[core, 0], (block, mirror, core),
+                vb_ref.at[pl.ds(0, direct_x), ys], recv_b.at[core, pl.ds(0, direct_x), ys],
+                b_send_sem.at[0, 0, part], b_recv_sem.at[core, 0, part], (block, mirror, core),
             ).wait_recv()
             remote(
-                relay.at[0], recv_b.at[core, pl.ds(direct_x, wide - direct_x)],
-                r_send_sem.at[0], b_recv_sem.at[core, 1], (1 - block, mirror, core),
+                relay.at[0, part], recv_b.at[core, pl.ds(direct_x, wide - direct_x), ys],
+                r_send_sem.at[0, part], b_recv_sem.at[core, 1, part], (1 - block, mirror, core),
             ).wait_recv()
-        for x in range(wide):
-            view_b[x, pl.ds(mine, tall)] = recv_b[gy, wide - 1 - x]
-
-    for x in range(wide):
-        view_b[x, pl.ds(other, tall)] = recv_b[1 - gy, wide - 1 - x]
+            for x in range(wide):
+                view_b[x, core * tall + BAND * part:core * tall + BAND * (part + 1)] = recv_b[core, wide - 1 - x, ys]
 
     outer = jnp.where(gy == 0, slab > 0, slab < devices - 1)
     neighbour = device_of(jnp.clip(slab + 2 * gy - 1, 0, devices - 1))
@@ -317,6 +331,7 @@
         blurred[x, ys] = total
 
     for part in range(side_bands):
+        pl.when(crossed)(functools.partial(crossed_view, part))
         for hop in range(1, devices):
             copy_a(part, hop).wait_recv()
         for side in range(2):
@@ -338,14 +353,22 @@
 
     def along_zy(values, index):
         high, low = split(values.reshape(chunks * LANES, full_z))
-        zh = tz_high[index]
-        done = dot(high, zh) + (dot(low, zh) + dot(high, tz_low[index]))
-        high, low = split(done)
-        yh, yl = ty_high[index], ty_low[index]
+        both = dot(jnp.concatenate([high, low], axis=1), table_z[index])
+        high, low = split(both[:, :LANES] + both[:, LANES:])
         outs = []
-        for chunk in range(chunks):
-            rows = slice(chunk * LANES, (chunk + 1) * LANES)
-            outs.append(dot(yh, high[rows]) + (dot(yh, low[rows]) + dot(yl, high[rows])))
+        for chunk in range(0, chunks, 2):
+            first = slice(chunk * LANES, (chunk + 1) * LANES)
+            second = slice((chunk + 1) * LANES, (chunk + 2) * LANES)
+            stacked = jnp.concatenate(
+                [
+                    jnp.concatenate([high[first], high[second]], axis=1),
+                    jnp.concatenate([low[first], low[second]], axis=1),
+                ],
+                axis=0,
+            )
+            both = dot(table_y[index], stacked)
+            both = both[:LANES] + both[LANES:]
+            outs += [both[:, :LANES], both[:, LANES:]]
         return jnp.concatenate(outs, axis=0).reshape(wide // 2, full_y, full_z)
 
     def middle(turn, which, view):
@@ -442,15 +465,17 @@
 
     @pl.when(crossed)
     def _():
-        for core in range(2):
-            detour(core).wait_send()
-            direct(core).wait_send()
+        for part in range(side_bands):
+            for core in range(2):
+                detour(core, part).wait_send()
+                direct(core, part).wait_send()
 
     @pl.when(jnp.logical_not(crossed))
     def _():
         half.wait_send()
-        for core in range(2):
-            onward(core).wait_send()
+        for part in range(side_bands):
+            for core in range(2):
+                onward(core, part).wait_send()
 
     for turn in range(4):
         for band in range(bands):
@@ -482,20 +507,19 @@
             pltpu.VMEM((devices, rows_y, deep, LANES), f32),
             pltpu.VMEM((2, rows_y, full_z, LANES), f32),
             pltpu.VMEM((2, wide, tall, full_z), f32),
-            pltpu.VMEM((2, wide // 2, tall, full_z), f32),
+            pltpu.VMEM((2, halves, wide // 2, BAND, full_z), f32),
             volume, volume, volume, volume,
             pltpu.VMEM((4, wide + 2 * radius, full_y, full_z), f32),
             pltpu.VMEM((2, rows_y, full_z, LANES), f32),
             pltpu.VMEM((devices, rows_y, deep, LANES), f32),
-            pltpu.VMEM((4, full_z, full_z), bf16), pltpu.VMEM((4, full_z, full_z), bf16),
-            pltpu.VMEM((4, LANES, LANES), bf16), pltpu.VMEM((4, LANES, LANES), bf16),
-            dma((4,)), dma((halves, devices)), dma((halves, devices)), dma((2, 2)), dma((2, 2)), dma((2,)), dma((2,)),
+            pltpu.VMEM((4, 2 * full_z, 2 * full_z), bf16), pltpu.VMEM((4, 2 * LANES, 2 * LANES), bf16),
+            dma((4,)), dma((halves, devices)), dma((halves, devices)), dma((2, 2, halves)), dma((2, 2, halves)), dma((2, halves)), dma((2, halves)),
             dma((4, bands, 2)), dma((4, bands, 2)), dma((halves, devices)), dma((halves, devices)),
         ],
         compiler_params=pltpu.CompilerParams(
-            collective_id=0, has_side_effects=True, vmem_limit_bytes=56000000
+            collective_id=0, has_side_effects=True, vmem_limit_bytes=48 * 1024 * 1024
         ),
-    )(view_a, view_b_own, spread_a, spread_b)
+    )(*(pltpu.with_memory_space_constraint(x, pltpu.HBM) for x in (view_a, view_b_own, spread_a, spread_b)))
     return jnp.transpose(turned, (1, 0, 2))
 
 

time: 55.5 us -> 51.6 us (0.930)
  Pallas kernels: 52.8 us -> 50.4 us
  local copies, waits for them, and re-layouts: 2.46 us -> 1.1 us
    pallas_call x1, Pallas kernels: 52.8 us -> 50.4 us  [slab_shards(): pl.pallas_call(deconvolve, out_shape=jax.ShapeDtypeStruct((tall, deep, lo...]
    unnamed x4 -> x0, local copies, waits for them, and re-layouts: 1.36 us -> none
where the time goes in v3:
time: 51.6 us; the launch traced here: 51.5 us
  Pallas kernels  50.4 us (98%)
  local copies, waits for them, and re-layouts  1.1 us (2%)
    pallas_call x1, Pallas kernels, slab_shards(): pl.pallas_call(deconvolve, out_shape=jax.ShapeDtypeStruct((tall, deep, lo...  50.4 us
    transpose x1, local copies, waits for them, and re-layouts, slab_shards(): return jnp.transpose(turned, (1, 0, 2))  1.1 us

profile of v3, /device:TPU:1, one launch (start us, length us, event | category | flops | bytes accessed | tf_op | source)
XLA Modules:
  0.0 51.5 jit_solution(16840852313241824596)
XLA Ops:
  0.0 50.4 %shard_map.46 = f32[16,16,512]{2,1,0:T(8,128)S(1)} custom-call(f32[16,16,512]{2,1,0:T(8,128)} %va_hbm.1, f32[64,16,128]{2,1,0:T(8,128)} %vb_hbm.1, f32[3,31]{1,0:T(4,128)} %sa_hbm.1, f32[3,31]{1,0:T(4,128)} %sb_hbm.1), custom_call_target="tpu_custom_call" | custom-call | tf_op jit(solution)/shard_map/pallas_call | solution.py:499
  50.4 1.1 %copy.5 = f32[16,16,512]{2,1,0:T(8,128)} copy(f32[16,16,512]{2,0,1:T(8,128)S(1)} %bitcast.1) | data formatting | bytes 1048576 | tf_op jit(solution)/shard_map/transpose | solution.py:523

commit v4 on v3

--- a/solution.py
+++ b/solution.py
@@ -332,14 +332,14 @@
 
     for part in range(side_bands):
         pl.when(crossed)(functools.partial(crossed_view, part))
-        for hop in range(1, devices):
-            copy_a(part, hop).wait_recv()
         for side in range(2):
+            for group in range(groups):
+                hop = lax.rem(me - 2 * group - side + devices, devices)
+                pl.when(hop != 0)(copy_a(part, hop).wait_recv)
             for y in range(lines * part, lines * (part + 1)):
                 turned = recv_a[side, y].T
                 for q in range(QUARTERS):
                     view_a[:, side * tall + QUARTERS * y + q, :] = turned[q * wide:(q + 1) * wide]
-        for side in range(2):
             band = side * side_bands + part
             ys = pl.ds(band * BAND, BAND)
             start = 0.5 * (view_a[:, ys] + view_b[:, ys])
@@ -423,7 +423,7 @@
         estimate[x, ys] = estimate[x, ys] * total
 
     def copy_e(side, part, step):
-        target = 2 * lax.rem(gz + step, groups) + side
+        target = 2 * step + side
         hop = lax.rem(target - me + devices, devices)
         rows = pl.ds(lines * part, lines)
         return remote(
@@ -431,6 +431,7 @@
             e_send_sem.at[part, hop], e_recv_sem.at[part, hop], at(target),
         )
 
+    far = gz >= groups // 2
     for band in order:
         side, part = band // side_bands, band % side_bands
         await_halos(3, band)
@@ -438,30 +439,46 @@
         for y in range(lines * part, lines * (part + 1)):
             strips = [estimate[:, side * tall + QUARTERS * y + q, :] for q in range(QUARTERS)]
             send_e[side, y] = jnp.concatenate(strips, axis=0).T
-        for step in range(1, groups):
-            copy_e(side, part, step).start()
-        pl.when(gy != side)(copy_e(side, part, 0).start)
+        for step in range(groups):
+            now = jnp.logical_not(far) if 2 <= step < groups // 2 else True
+            pl.when(jnp.logical_and(me != 2 * step + side, now))(copy_e(side, part, step).start)
+
+    @pl.when(far)
+    def _():
+        for band in order:
+            for step in range(2, groups // 2):
+                copy_e(band // side_bands, band % side_bands, step).start()
 
     recv_e[slab] = send_e[gy, :, own_z]
+    columns = long_x // LANES
+
+    def arrived_e(part, place):
+        source = 2 * snake(groups - 1 - place // 2) + lax.rem(place, 2)
+        hop = lax.rem(me - source + devices, devices)
+        pl.when(hop != 0)(
+            remote(
+                send_e.at[0, pl.ds(0, lines), pl.ds(0, deep)], recv_e.at[place, pl.ds(lines * part, lines)],
+                e_send_sem.at[part, hop], e_recv_sem.at[part, hop], at(lax.rem(me + hop, devices)),
+            ).wait_recv
+        )
+
     for part in range(side_bands):
-        for hop in range(1, devices):
-            remote(
-                send_e.at[0, pl.ds(0, lines), pl.ds(0, deep)], recv_e.at[slab, pl.ds(lines * part, lines)],
-                e_send_sem.at[part, hop], e_recv_sem.at[part, hop], at(lax.rem(me + hop, devices)),
-            ).wait_recv()
-        for y in range(lines * part, lines * (part + 1)):
-            for column in range(long_x // LANES):
+        for step in range(columns):
+            column = jnp.where(gz < groups // 2, columns - 1 - step, step)
+            xs = pl.ds(pl.multiple_of(column * LANES, LANES), LANES)
+            for k in range(QUARTERS):
+                arrived_e(part, QUARTERS * column + k)
+            for y in range(lines * part, lines * (part + 1)):
                 pieces = [recv_e[QUARTERS * column + k, y] for k in range(QUARTERS)]
                 for q, piece in enumerate(block_transpose(pieces, wide)):
-                    out_ref[QUARTERS * y + q, :, column * LANES:(column + 1) * LANES] = piece
+                    out_ref[QUARTERS * y + q, :, xs] = piece
 
     for part in range(side_bands):
         for hop in range(1, devices):
             copy_a(part, hop).wait_send()
         for side in range(2):
-            for step in range(1, groups):
-                copy_e(side, part, step).wait_send()
-            pl.when(gy != side)(copy_e(side, part, 0).wait_send)
+            for step in range(groups):
+                pl.when(me != 2 * step + side)(copy_e(side, part, step).wait_send)
 
     @pl.when(crossed)
     def _():

time: 51.6 us -> 50.6 us (0.981)
  the two profiles are of different devices: /device:TPU:1 before, /device:TPU:15 now
where the time goes in v4:
time: 50.6 us; the launch traced here: 50.5 us
  Pallas kernels  49.3 us (97%)
  local copies, waits for them, and re-layouts  1.1 us (2%)
    pallas_call x1, Pallas kernels, slab_shards(): pl.pallas_call(deconvolve, out_shape=jax.ShapeDtypeStruct((tall, deep, lo...  49.3 us
    transpose x1, local copies, waits for them, and re-layouts, slab_shards(): return jnp.transpose(turned, (1, 0, 2))  1.1 us

profile of v4, /device:TPU:15, one launch (start us, length us, event | category | flops | bytes accessed | tf_op | source)
XLA Modules:
  0.0 50.5 jit_solution(963775062994243088)
XLA Ops:
  0.0 49.3 %shard_map.46 = f32[16,16,512]{2,1,0:T(8,128)S(1)} custom-call(f32[16,16,512]{2,1,0:T(8,128)} %va_hbm.1, f32[64,16,128]{2,1,0:T(8,128)} %vb_hbm.1, f32[3,31]{1,0:T(4,128)} %sa_hbm.1, f32[3,31]{1,0:T(4,128)} %sb_hbm.1), custom_call_target="tpu_custom_call" | custom-call | tf_op jit(solution)/shard_map/pallas_call | solution.py:516
  49.4 1.1 %copy.5 = f32[16,16,512]{2,1,0:T(8,128)} copy(f32[16,16,512]{2,0,1:T(8,128)S(1)} %bitcast.1) | data formatting | bytes 1048576 | tf_op jit(solution)/shard_map/transpose | solution.py:540

commit v5 on v4

--- a/solution.py
+++ b/solution.py
@@ -407,11 +407,11 @@
         x_taps(1, 0, 1, band, True, update)
         send_outer(2, band)
         send_inner(2, band)
+
+    looped(second_edges)
+
+    def third_edges(band):
         x_taps(2, 1, 0, band, False, keep)
-
-    looped(second_edges)
-
-    def third_edges(band):
         await_halos(2, band)
         x_taps(2, 1, 0, band, True, keep)
 

time: 50.6 us -> 50.6 us (level)
  no operation moved by 1% of the time
where the time goes in v5:
time: 50.6 us; the launch traced here: 50.5 us
  Pallas kernels  49.3 us (97%)
  local copies, waits for them, and re-layouts  1.1 us (2%)
    pallas_call x1, Pallas kernels, slab_shards(): pl.pallas_call(deconvolve, out_shape=jax.ShapeDtypeStruct((tall, deep, lo...  49.3 us
    transpose x1, local copies, waits for them, and re-layouts, slab_shards(): return jnp.transpose(turned, (1, 0, 2))  1.1 us

profile of v5, /device:TPU:15, one launch (start us, length us, event | category | flops | bytes accessed | tf_op | source)
XLA Modules:
  0.0 50.5 jit_solution(13820147321500492461)
XLA Ops:
  0.0 49.3 %shard_map.46 = f32[16,16,512]{2,1,0:T(8,128)S(1)} custom-call(f32[16,16,512]{2,1,0:T(8,128)} %va_hbm.1, f32[64,16,128]{2,1,0:T(8,128)} %vb_hbm.1, f32[3,31]{1,0:T(4,128)} %sa_hbm.1, f32[3,31]{1,0:T(4,128)} %sb_hbm.1), custom_call_target="tpu_custom_call" | custom-call | tf_op jit(solution)/shard_map/pallas_call | solution.py:516
  49.4 1.1 %copy.5 = f32[16,16,512]{2,1,0:T(8,128)} copy(f32[16,16,512]{2,0,1:T(8,128)S(1)} %bitcast.1) | data formatting | bytes 1048576 | tf_op jit(solution)/shard_map/transpose | solution.py:540
